TPU v7x, 128 devices: a whole 4x4x4 slice. The times are simulated.
128 devices in a mesh: branch: 4 (over z_lo, core), shard: 32 (over y, x, z_hi).
Axes of the slice: x: 4, y: 4, z: 4 (z_hi: 2, z_lo: 2; z = z_hi * 2 + z_lo), core: 2. Of those that a mesh axis runs over, the one named last changes fastest.
Arguments:
- attention_weights: bfloat16 [4, 2, 4096, 4096], P('branch', None, None, 'shard'), may hold values from -1.25 to 1.25
- ffn_weights: bfloat16 [4, 3, 4096, 11008], P('branch', None, 'shard'), may hold values from -0.3125 to 0.3125
- tokens: bfloat16 [2048, 4096], P(('branch', 'shard')), may hold values from -6 to 6
- routes: int32 [2048, 2], P(('branch', 'shard')), may hold values from 0 to 3, all different within a row; in each aligned block of 16 rows (0 to 15, 16 to 31, ...) at most 12 rows name the same one
- router: bfloat16 [4096, 4], replicated, may hold values from -0.09375 to 0.09375
Outputs:
- merged_attention: bfloat16 [2, 4096, 4096], P(None, 'branch', 'shard')
- expert_weights: bfloat16 [4, 3, 4096, 11008], P('branch', None, None, 'shard')
- mixed_output: bfloat16 [2048, 4096], P(('branch', 'shard'))
Inputs may be any that keep to these rules, and one draw needn't show every extreme that they name: `routes`: the 2 experts of a row differ. In each aligned block of 16 rows (the rows of one device) no expert is named by more than 12 rows, and in some blocks one expert is named by exactly 12 rows.
All inputs are finite; a program needn't handle non-finite values.
Results may differ from a plain program's by a relative error of at most 0.018.
Values may be sent and summed in bfloat16 or wider, within the bound.
A program may use at most 192 MiB of HBM per device.

v0:
```python
import jax
import jax.numpy as jnp
from jax import lax
from jax.sharding import Mesh
from jax.sharding import PartitionSpec as P

SHARD = ("shard_0", "shard_1", "shard_2")
BRANCH_SHARD = ("branch", "shard_0", "shard_1", "shard_2")


def own_rows(terms, axes):
    running = terms.astype(jnp.bfloat16)
    for axis in axes:
        running = lax.psum_scatter(running, axis, scatter_dimension=0, tiled=True)
    return running.astype(jnp.float32)


def slot_table(route_rows, experts_count, capacity):
    chosen = (route_rows[:, :, None] == jnp.arange(experts_count, dtype=jnp.int32)).astype(
        jnp.int32
    )
    flat_picks = chosen.reshape(-1, experts_count)
    before = jnp.cumsum(flat_picks, axis=0) - flat_picks
    position = jnp.sum(before * flat_picks, axis=1)
    slot_id = route_rows.reshape(-1) * capacity + position
    one_hot = (slot_id[:, None] == jnp.arange(experts_count * capacity, dtype=jnp.int32)).astype(
        jnp.float32
    )
    return jnp.sum(one_hot.reshape(route_rows.shape[0], route_rows.shape[1], -1), axis=1)


def local(attention_weights, ffn_weights, tokens, routes, router):
    branches = lax.axis_size("branch")
    expert_weights = lax.all_to_all(ffn_weights, SHARD, split_axis=3, concat_axis=2, tiled=True)
    gate_weight = expert_weights[0, 0]
    up_weight = expert_weights[0, 1]
    down_weight = expert_weights[0, 2]
    tok_count = tokens.shape[0]
    model_width = tokens.shape[1]
    capacity = 3 * tok_count // 4
    slot_map = slot_table(routes, branches, capacity)
    buffers = lax.dot_general(
        slot_map.astype(jnp.bfloat16),
        tokens,
        (((0,), (0,)), ((), ())),
        preferred_element_type=jnp.float32,
    )
    buffers = buffers.astype(jnp.bfloat16).reshape(branches, capacity, model_width)
    arrived = lax.all_to_all(buffers, "branch", split_axis=0, concat_axis=0, tiled=True)
    slot_rows = lax.all_gather(
        arrived.reshape(branches * capacity, model_width), SHARD, axis=0, tiled=True
    )
    gate_proj = jnp.dot(slot_rows, gate_weight, preferred_element_type=jnp.float32)
    up_proj = jnp.dot(slot_rows, up_weight, preferred_element_type=jnp.float32)
    hidden = (jax.nn.silu(gate_proj) * up_proj).astype(jnp.bfloat16)
    summed = own_rows(
        lax.dot_general(
            hidden, down_weight, (((1,), (1,)), ((), ())), preferred_element_type=jnp.float32
        ),
        SHARD,
    )
    outputs = summed.astype(jnp.bfloat16).reshape(branches, capacity, model_width)
    returned = lax.all_to_all(outputs, "branch", split_axis=0, concat_axis=0, tiled=True)
    gates_all = jax.nn.sigmoid(jnp.dot(tokens, router, preferred_element_type=jnp.float32))
    weighting = slot_map * jnp.repeat(gates_all, capacity, axis=1)
    mixed_output = jnp.dot(
        weighting, returned.reshape(branches * capacity, model_width).astype(jnp.float32)
    )
    mixed_output = mixed_output.astype(jnp.bfloat16)
    traded = lax.all_to_all(attention_weights, "branch", split_axis=2, concat_axis=0, tiled=True)
    summed_attention = jnp.sum(traded.astype(jnp.float32), axis=0)
    merged_attention = (summed_attention * (1.0 / branches)).astype(jnp.bfloat16)
    return (merged_attention, expert_weights, mixed_output)


def solution(mesh):
    torus = Mesh(
        mesh.devices.reshape(mesh.shape["branch"], 4, 4, 2),
        ("branch", "shard_0", "shard_1", "shard_2"),
    )
    in_specs = (
        P("branch", None, None, SHARD),
        P("branch", None, SHARD, None),
        P(BRANCH_SHARD, None),
        P(BRANCH_SHARD, None),
        P(),
    )
    out_specs = (P(None, "branch", SHARD), P("branch", None, None, SHARD), P(BRANCH_SHARD, None))
    return jax.shard_map(local, mesh=torus, in_specs=in_specs, out_specs=out_specs, check_vma=False)
```

profile of v0, /device:TPU:1, one launch (start us, length us, event | category | flops | bytes accessed | tf_op | source)
XLA Modules:
  0.0 518.2 jit_solution(2717877055317344785)
XLA Ops:
  7.2 0.0 copy-start
  7.2 0.0 all-gather.2.cloned.1.call-start
  7.2 0.8 copy.58
  8.0 0.1 eq.30
  8.1 0.1 fusion.13
  8.2 0.1 reduce_window_sum.11
  8.2 0.2 select_reduce_fusion
  8.4 0.1 reduce_sum.33
  8.5 0.1 copy.59
  8.6 0.7 multiply_add_fusion
  9.3 0.1 convert_reduce_fusion.1
  9.4 0.0 copy-done
  9.4 0.3 convolution_convert_fusion.1
  9.7 0.1 reshape.45
  9.8 12.2 %all_to_all.37 = bf16[4,12,4096]{2,1,0:T(8,128)(2,1)S(1)} all-to-all(bf16[4,12,4096]{2,1,0:T(8,128)(2,1)S(1)} %reshape.45), channel_id=1, replica_groups=mesh['branch'=4,'shard_0'=4,'shard_1'=4,'shard_2'=2] {'branch'}, dimensions={0} | all-to-all | bytes 786432 | tf_op jit(solution)/shard_map/all_to_all | solution.py:49
  22.0 0.8 reshape.46
  22.8 0.0 all-gather.2.cloned.1.call-update
  22.9 0.0 reduce-scatter.4.cloned.1.call-start
  22.9 17.6 %copy.55 = bf16[1,3,128,11008]{2,1,0,3:T(4,128)(2,1)} copy(bf16[1,3,128,11008]{3,2,1,0:T(8,128)(2,1)} %param.6) | data formatting | bytes 16908288 | tf_op args[1]
  40.5 145.7 %all_to_all.38 = bf16[1,3,128,11008]{2,1,0,3:T(4,128)(2,1)S(1)} all-to-all(bf16[1,3,128,11008]{2,1,0,3:T(4,128)(2,1)} %copy.55), channel_id=1, replica_groups=mesh['branch'=4,'shard_0'=4,'shard_1'=4,'shard_2'=2] {'shard_0','shard_1..., dimensions={3} | all-to-all | bytes 16908288 | tf_op jit(solution)/shard_map/all_to_all | solution.py:34
  186.2 5.0 copy.56
  191.3 9.2 %copy.67 = bf16[1,3,32,43,8,128]{5,4,2,3,1,0:T(8,128)(2,1)} copy(bf16[1,3,32,43,8,128]{5,4,3,2,1,0:T(8,128)(2,1)} %bitcast.32) | data formatting | bytes 16908288 | tf_op jit(solution)/shard_map/all_to_all | solution.py:34
  200.4 67.3 %all-gather.2.cloned.1.call-done = bf16[1536,4096]{1,0:T(8,128)(2,1)} async-done(((bf16[48,4096]{1,0:T(8,128)(2,1)}), bf16[1536,4096]{1,0:T(8,128)(2,1)}) %all-gather.2.cloned.1.call-update) | async-done | bytes 12582928 | tf_op jit(solution)/shard_map/all_gather | solution.py:50
  267.7 8.5 %fusion.1 = f32[1536,344]{0,1:T(8,128)S(1)} fusion(bf16[1536,4096]{1,0:T(8,128)(2,1)} %all-gather.2.cloned.1.call-done, bf16[1,3,4096,344]{2,3,1,0:T(8,128)(2,1)} %bitcast.33), kind=kOutput, calls=%fused_computation.10 | convolution fusion | flops 4328521728 | bytes 17514496 | tf_op jit(solution)/shard_map/dot_general | solution.py:53
  276.2 21.6 %convolution_convert_fusion = bf16[1536,4096]{1,0:T(8,128)(2,1)} fusion(bf16[1,3,4096,344]{2,3,1,0:T(8,128)(2,1)} %bitcast.34, bf16[1536,4096]{1,0:T(8,128)(2,1)} %all-gather.2.cloned.1.call-done, f32[1536,344]{0,1:T(8,128)S(1)} %fusion.1), kind=kOutput, calls=%fused_computation | convolution fusion | flops 8666505216 | bytes 32915456 | tf_op jit(solution)/shard_map/dot_general | solution.py:57
  297.7 0.0 reduce-scatter.4.cloned.1.call-update
  297.7 0.0 copy-start.1
  297.8 0.0 reduce-scatter.6.cloned.1.call-start
  297.8 113.0 %reduce-scatter.4.cloned.1.call-done = bf16[384,4096]{1,0:T(8,128)(2,1)} async-done(((bf16[1536,4096]{1,0:T(8,128)(2,1)}), bf16[384,4096]{1,0:T(8,128)(2,1)}) %reduce-scatter.4.cloned.1.call-update) | async-done | bytes 3145744 | tf_op jit(solution)/shard_map/reduce_scatter | solution.py:14
  410.8 0.0 reduce-scatter.6.cloned.1.call-update
  410.8 0.2 reduce-scatter.8.cloned.1.call-start
  411.0 40.1 %reduce-scatter.6.cloned.1.call-done = bf16[96,4096]{1,0:T(8,128)(2,1)} async-done(((bf16[384,4096]{1,0:T(8,128)(2,1)}), bf16[96,4096]{1,0:T(8,128)(2,1)}) %reduce-scatter.6.cloned.1.call-update) | async-done | bytes 786448 | tf_op jit(solution)/shard_map/reduce_scatter | solution.py:14
  451.2 0.0 reduce-scatter.8.cloned.1.call-update
  451.2 0.0 copy-done.1
  451.2 18.1 %copy.54 = bf16[1,2,4096,128]{3,1,0,2:T(2,128)(2,1)} copy(bf16[1,2,4096,128]{3,2,1,0:T(8,128)(2,1)S(1)} %copy-done.1) | data formatting | bytes 4194304 | tf_op args[0]
  469.3 0.0 copy-start.2
  469.3 4.4 all-to-all-start
  473.8 0.1 reduce_sum.35
  473.8 0.0 copy-done.2
  473.9 0.2 fusion.10
  474.0 0.1 copy.60
  474.1 0.1 broadcast_multiply_fusion
  474.2 0.5 reduce-scatter.8.cloned.1.call-done
  474.8 1.9 reshape.47
  476.6 21.8 %all-to-all-done = bf16[1,2,4096,128]{3,1,0,2:T(2,128)(2,1)S(1)} async-done(((bf16[1,2,4096,128]{3,1,0,2:T(2,128)(2,1)}), bf16[1,2,4096,128]{3,1,0,2:T(2,128)(2,1)S(1)}, u32[]{:S(2)}, u32[]{:S(2)}) %all-to-all-start) | async-done | bytes 2097184 | tf_op jit(solution)/shard_map/all_to_all | solution.py:70
  498.5 4.4 all-to-all-start.3
  502.9 2.1 convert_reduce_fusion
  505.0 0.5 multiply_convert_fusion
  505.5 0.9 copy.62
  506.3 4.4 all-to-all-done.3
  510.7 1.0 fusion
Async XLA Ops:
  7.2 2.2 copy-start
  7.2 260.5 %all-gather.2.cloned.1.call-start = ((), (), s32[]{:S(2)}) async-start(), calls=%async_computation.7 | async-start | bytes 12976128 | tf_op jit(solution)/shard_map/all_gather | solution.py:50
  22.9 387.9 %reduce-scatter.4.cloned.1.call-start = ((), (), s32[]{:S(2)}) async-start(), calls=%async_computation.8 | async-start | bytes 15728640 | tf_op jit(solution)/shard_map/reduce_scatter | solution.py:14
  297.7 153.4 %copy-start.1 = (bf16[1,2,4096,128]{3,2,1,0:T(8,128)(2,1)S(1)}, bf16[1,2,4096,128]{3,2,1,0:T(8,128)(2,1)}, u32[]{:S(2)}) copy-start(bf16[1,2,4096,128]{3,2,1,0:T(8,128)(2,1)} %param.5) | copy-start | bytes 6291460
  297.8 153.4 %reduce-scatter.6.cloned.1.call-start = ((), (), s32[]{:S(2)}) async-start(), calls=%async_computation.9 | async-start | bytes 3932160 | tf_op jit(solution)/shard_map/reduce_scatter | solution.py:14
  410.8 64.0 %reduce-scatter.8.cloned.1.call-start = ((), (), s32[]{:S(2)}) async-start(), calls=%async_computation.10 | async-start | bytes 1179648 | tf_op jit(solution)/shard_map/reduce_scatter | solution.py:14
  469.3 4.5 copy-start.2
  469.3 29.1 %all-to-all-start = ((bf16[1,2,4096,128]{3,1,0,2:T(2,128)(2,1)}), bf16[1,2,4096,128]{3,1,0,2:T(2,128)(2,1)S(1)}, u32[]{:S(2)}, u32[]{:S(2)}) async-start(bf16[1,2,4096,128]{3,1,0,2:T(2,128)(2,1)} %copy.54), calls=%async_computation | async-start | bytes 4194304 | tf_op jit(solution)/shard_map/all_to_all | solution.py:70
  498.5 12.3 %all-to-all-start.3 = ((bf16[4,12,4096]{2,1,0:T(8,128)(2,1)}), bf16[4,12,4096]{2,1,0:T(8,128)(2,1)S(1)}, u32[]{:S(2)}, u32[]{:S(2)}) async-start(bf16[4,12,4096]{2,1,0:T(8,128)(2,1)} %reshape.47), calls=%async_computation.6 | async-start | bytes 1048576 | tf_op jit(solution)/shard_map/all_to_all | solution.py:63
Sparse Core Ops, SparseCore 0:
  23.0 244.6 all-gather.1
  297.9 112.8 reduce-scatter.3
  413.2 37.9 reduce-scatter.5
  453.4 21.3 reduce-scatter.7
where the time goes:
time: 519 us; the launch traced here: 518 us
  waiting for transfers between devices  247 us (48%)
  blocking collectives  158 us (30%)
  local copies, waits for them, and re-layouts  54.8 us (11%)
  matrix products  31.4 us (6%)
  between operations  13.9 us (3%)
  starting transfers between devices  9.18 us (2%)
    reduce_scatter x3, waiting for transfers between devices, own_rows(): running = lax.psum_scatter(running, axis, scatter_dimension=0, tiled=True)  154 us
    all_to_all x1, blocking collectives, local(): lax.all_to_all(ffn_weights, SHARD, split_axis=3, concat_axis=2, tiled=True)  146 us
    all_gather x1, waiting for transfers between devices, local(): lax.all_gather(arrived.reshape(branches * capacity, model_width), SHARD,...  67.3 us
    unnamed x10, local copies, waits for them, and re-layouts  37.4 us
    all_to_all x1, waiting for transfers between devices, local(): lax.all_to_all(attention_weights, 'branch', split_axis=2, concat_axis=0,...  21.8 us
    dot_general x1, matrix products, local(): lax.dot_general(hidden, down_weight, (((1,), (1,)), ((), ())), preferred_...  21.6 us
    all_to_all x2, local copies, waits for them, and re-layouts, local(): lax.all_to_all(ffn_weights, SHARD, split_axis=3, concat_axis=2, tiled=True)  14.2 us
    all_to_all x1, blocking collectives, local(): lax.all_to_all(buffers, 'branch', split_axis=0, concat_axis=0, tiled=True)  12.2 us
  transfers between devices with their start and end apart: 6, of which 6 were waited for; matrix products, arithmetic and copies ran while one was open for 11% of the time, Pallas kernels for 0%

commit v1 on v0

--- a/solution.py
+++ b/solution.py
@@ -31,7 +31,12 @@
 
 def local(attention_weights, ffn_weights, tokens, routes, router):
     branches = lax.axis_size("branch")
-    expert_weights = lax.all_to_all(ffn_weights, SHARD, split_axis=3, concat_axis=2, tiled=True)
+    expert_weights = jnp.concatenate(
+        lax.all_to_all(
+            jnp.stack(jnp.split(ffn_weights, lax.axis_size(SHARD), axis=3)), SHARD, 0, 0
+        ),
+        axis=2,
+    )
     gate_weight = expert_weights[0, 0]
     up_weight = expert_weights[0, 1]
     down_weight = expert_weights[0, 2]

time: 519 us -> 496 us (0.956)
  local copies, waits for them, and re-layouts: 54.8 us -> 90.3 us
  waiting for transfers between devices: 247 us -> 216 us
  blocking collectives: 158 us -> 130 us
    all_gather x1, waiting for transfers between devices: 67.3 us -> 36.1 us  [local(): lax.all_gather(arrived.reshape(branches * capacity, model_width), SHARD,...]
    unnamed x10 -> x100, local copies, waits for them, and re-layouts: 37.4 us -> 66 us
    all_to_all x1, blocking collectives: 146 us -> 118 us  [local(): lax.all_to_all(jnp.stack(jnp.split(ffn_weights, lax.axis_size(SHARD), axi...]
    all_to_all x2 -> x0, local copies, waits for them, and re-layouts: 14.2 us -> none  [local(): lax.all_to_all(ffn_weights, SHARD, split_axis=3, concat_axis=2, tiled=True)]
    split x0 -> x2, local copies, waits for them, and re-layouts: none -> 13 us  [local(): jnp.split(ffn_weights, lax.axis_size(SHARD), axis=3)]
    reshape x0 -> x1, local copies, waits for them, and re-layouts: none -> 8 us  [local(): jnp.concatenate(lax.all_to_all(jnp.stack(jnp.split(ffn_weights, lax.axis_...]
  transfers between devices with their start and end apart: 6 -> 6, of which waited for: 6 -> 6; matrix products, arithmetic and copies ran while one was open for 11% -> 18% of each run, Pallas kernels for 0% -> 0%
where the time goes in v1:
time: 496 us; the launch traced here: 495 us
  waiting for transfers between devices  216 us (44%)
  blocking collectives  130 us (26%)
  local copies, waits for them, and re-layouts  90.3 us (18%)
  matrix products  31.4 us (6%)
  between operations  14.3 us (3%)
  starting transfers between devices  9.09 us (2%)
    reduce_scatter x3, waiting for transfers between devices, own_rows(): running = lax.psum_scatter(running, axis, scatter_dimension=0, tiled=True)  154 us
    all_to_all x1, blocking collectives, local(): lax.all_to_all(jnp.stack(jnp.split(ffn_weights, lax.axis_size(SHARD), axi...  118 us
    unnamed x100, local copies, waits for them, and re-layouts  66 us
    all_gather x1, waiting for transfers between devices, local(): lax.all_gather(arrived.reshape(branches * capacity, model_width), SHARD,...  36.1 us
    all_to_all x1, waiting for transfers between devices, local(): lax.all_to_all(attention_weights, 'branch', split_axis=2, concat_axis=0,...  21.7 us
    dot_general x1, matrix products, local(): lax.dot_general(hidden, down_weight, (((1,), (1,)), ((), ())), preferred_...  21.6 us
    split x2, local copies, waits for them, and re-layouts, local(): jnp.split(ffn_weights, lax.axis_size(SHARD), axis=3)  13 us
    all_to_all x1, blocking collectives, local(): lax.all_to_all(buffers, 'branch', split_axis=0, concat_axis=0, tiled=True)  12.2 us
  transfers between devices with their start and end apart: 6, of which 6 were waited for; matrix products, arithmetic and copies ran while one was open for 18% of the time, Pallas kernels for 0%

profile of v1, /device:TPU:1, one launch (start us, length us, event | category | flops | bytes accessed | tf_op | source)
XLA Modules:
  0.0 495.3 jit_solution(4587957319680748992)
XLA Ops:
  7.2 0.8 copy.209
  8.6 0.7 multiply_add_fusion
  9.4 0.3 convolution_convert_fusion.1
  9.8 12.2 %all_to_all.24 = bf16[4,12,4096]{2,1,0:T(8,128)(2,1)S(1)} all-to-all(bf16[4,12,4096]{2,1,0:T(8,128)(2,1)S(1)} %reshape.53), channel_id=1, replica_groups=mesh['branch'=4,'shard_0'=4,'shard_1'=4,'shard_2'=2] {'branch'}, dimensions={0} | all-to-all | bytes 786432 | tf_op jit(solution)/shard_map/all_to_all | solution.py:54
  22.0 0.8 reshape.54
  22.9 5.3 %fusion.17 = (bf16[1,3,128,344]{3,2,1,0:T(8,128)(2,1)S(1)}, bf16[1,3,128,344]{3,2,1,0:T(8,128)(2,1)S(1)}, bf16[1,3,128,344]{3,2,1,0:T(8,128)(2,1)S(1)}, bf16[1,3...) fusion(bf16[1,3,128,11008]{3,2,1,0:T(8,128)(2,1)} %param.6), kind=kLoop, calls=%fused_computation.66 | loop fusion | bytes 6868992 | tf_op jit(solution)/shard_map/split | solution.py:36
  28.2 1.8 copy.214
  30.0 1.8 copy.215
  31.9 0.9 copy.216
  32.7 0.9 copy.217
  33.6 0.9 copy.218
  34.5 0.9 copy.219
  35.4 0.9 copy.220
  36.3 0.9 copy.221
  37.1 0.9 copy.222
  38.0 0.9 copy.223
  38.9 0.9 copy.224
  39.7 0.9 copy.225
  40.6 0.9 copy.226
  41.5 7.7 %fusion.16 = (bf16[1,3,128,344]{3,2,1,0:T(8,128)(2,1)S(1)}, bf16[1,3,128,344]{3,2,1,0:T(8,128)(2,1)S(1)}, bf16[1,3,128,344]{3,2,1,0:T(8,128)(2,1)S(1)}, bf16[1,3...) fusion(bf16[1,3,128,11008]{3,2,1,0:T(8,128)(2,1)} %param.6), kind=kLoop, calls=%fused_computation.65 | loop fusion | bytes 10039296 | tf_op jit(solution)/shard_map/split | solution.py:36
  49.2 1.8 copy.227
  51.0 1.8 copy.228
  52.8 1.8 copy.229
  54.6 1.8 copy.230
  56.5 1.8 copy.231
  58.3 1.8 copy.232
  60.1 1.8 copy.233
  62.0 1.8 copy.234
  63.8 0.9 copy.235
  64.7 0.9 copy.236
  65.6 0.9 copy.237
  66.4 0.9 copy.238
  67.3 0.9 copy.239
  69.5 1.1 bitcast_dynamic-update-slice_fusion.31
  70.6 1.0 bitcast_dynamic-update-slice_fusion.30
  71.6 1.0 bitcast_dynamic-update-slice_fusion.29
  72.6 1.0 bitcast_dynamic-update-slice_fusion.28
  73.6 1.0 bitcast_dynamic-update-slice_fusion.27
  74.6 1.0 bitcast_dynamic-update-slice_fusion.26
  75.6 1.0 bitcast_dynamic-update-slice_fusion.25
  76.6 1.0 bitcast_dynamic-update-slice_fusion.24
  77.6 1.0 bitcast_dynamic-update-slice_fusion.23
  78.8 1.0 bitcast_dynamic-update-slice_fusion.18
  79.8 1.0 bitcast_dynamic-update-slice_fusion.17
  80.8 1.0 bitcast_dynamic-update-slice_fusion.16
  82.6 118.2 %all_to_all.25 = bf16[32,1,3,128,344]{3,4,2,1,0:T(8,128)(2,1)} all-to-all(bf16[32,1,3,128,344]{3,4,2,1,0:T(8,128)(2,1)S(1)} %bitcast_dynamic-update-slice_fusion), channel_id=1, replica_groups=mesh['branch'=4,'shard_0'=4,'shard_1'=4,'shard_2'=2] {'shard_0','shard_1..., dimensions={0} | all-to-all | bytes 16908288 | tf_op jit(solution)/shard_map/all_to_all | solution.py:35
  200.8 8.0 %copy_bitcast_fusion = bf16[1,3,4096,344]{2,3,1,0:T(8,128)(2,1)} fusion(bf16[32,1,3,128,344]{3,4,2,1,0:T(8,128)(2,1)} %all_to_all.25), kind=kLoop, calls=%fused_computation.1 | loop fusion | bytes 16908288 | tf_op jit(solution)/shard_map/reshape | solution.py:34
  208.8 36.1 %all-gather.2.cloned.1.call-done = bf16[1536,4096]{1,0:T(8,128)(2,1)} async-done(((bf16[48,4096]{1,0:T(8,128)(2,1)}), bf16[1536,4096]{1,0:T(8,128)(2,1)}) %all-gather.2.cloned.1.call-update) | async-done | bytes 12582928 | tf_op jit(solution)/shard_map/all_gather | solution.py:55
  244.9 8.5 %fusion.1 = f32[1536,344]{0,1:T(8,128)S(1)} fusion(bf16[1536,4096]{1,0:T(8,128)(2,1)} %all-gather.2.cloned.1.call-done, bf16[1,3,4096,344]{2,3,1,0:T(8,128)(2,1)} %copy_bitcast_fusion), kind=kOutput, calls=%fused_computation.10 | convolution fusion | flops 4328521728 | bytes 17514496 | tf_op jit(solution)/shard_map/dot_general | solution.py:58
  253.4 21.6 %convolution_convert_fusion = bf16[1536,4096]{1,0:T(8,128)(2,1)} fusion(bf16[1,3,4096,344]{2,3,1,0:T(8,128)(2,1)} %copy_bitcast_fusion, bf16[1536,4096]{1,0:T(8,128)(2,1)} %all-gather.2.cloned.1.call-done, f32[1536,344]{0,1:T(8,128)S(1)} %fusion.1), kind=kOutput, calls=%fused_computation | convolution fusion | flops 8666505216 | bytes 32915456 | tf_op jit(solution)/shard_map/dot_general | solution.py:62
  275.0 113.0 %reduce-scatter.4.cloned.1.call-done = bf16[384,4096]{1,0:T(8,128)(2,1)} async-done(((bf16[1536,4096]{1,0:T(8,128)(2,1)}), bf16[384,4096]{1,0:T(8,128)(2,1)}) %reduce-scatter.4.cloned.1.call-update) | async-done | bytes 3145744 | tf_op jit(solution)/shard_map/reduce_scatter | solution.py:14
  388.0 0.3 reduce-scatter.8.cloned.1.call-start
  388.3 40.1 %reduce-scatter.6.cloned.1.call-done = bf16[96,4096]{1,0:T(8,128)(2,1)} async-done(((bf16[384,4096]{1,0:T(8,128)(2,1)}), bf16[96,4096]{1,0:T(8,128)(2,1)}) %reduce-scatter.6.cloned.1.call-update) | async-done | bytes 786448 | tf_op jit(solution)/shard_map/reduce_scatter | solution.py:14
  428.4 18.1 %copy.175 = bf16[1,2,4096,128]{3,1,0,2:T(2,128)(2,1)} copy(bf16[1,2,4096,128]{3,2,1,0:T(8,128)(2,1)S(1)} %copy-done.1) | data formatting | bytes 4194304 | tf_op args[0]
  446.5 4.3 all-to-all-start
  451.3 0.7 reduce-scatter.8.cloned.1.call-done
  452.0 1.9 reshape.55
  453.8 21.7 %all-to-all-done = bf16[1,2,4096,128]{3,1,0,2:T(2,128)(2,1)S(1)} async-done(((bf16[1,2,4096,128]{3,1,0,2:T(2,128)(2,1)}), bf16[1,2,4096,128]{3,1,0,2:T(2,128)(2,1)S(1)}, u32[]{:S(2)}, u32[]{:S(2)}) %all-to-all-start) | async-done | bytes 2097184 | tf_op jit(solution)/shard_map/all_to_all | solution.py:75
  475.5 4.4 all-to-all-start.3
  479.9 2.1 convert_reduce_fusion
  482.0 0.5 multiply_convert_fusion
  482.5 0.9 copy.213
  483.4 4.4 all-to-all-done.3
  487.8 1.0 fusion
  (79 shorter events, 3.4 us)
Async XLA Ops:
  7.2 2.2 copy-start
  7.2 237.7 %all-gather.2.cloned.1.call-start = ((), (), s32[]{:S(2)}) async-start(), calls=%async_computation.7 | async-start | bytes 12976128 | tf_op jit(solution)/shard_map/all_gather | solution.py:55
  22.9 365.1 %reduce-scatter.4.cloned.1.call-start = ((), (), s32[]{:S(2)}) async-start(), calls=%async_computation.8 | async-start | bytes 15728640 | tf_op jit(solution)/shard_map/reduce_scatter | solution.py:14
  64.7 14.0 %copy-start.2 = (bf16[1,3,128,344]{2,3,1,0:T(8,128)(2,1)S(1)}, bf16[1,3,128,344]{2,3,1,0:T(8,128)(2,1)}, u32[]{:S(2)}) copy-start(bf16[1,3,128,344]{2,3,1,0:T(8,128)(2,1)} %copy.225) | copy-start | bytes 792580
  65.6 13.2 %copy-start.3 = (bf16[1,3,128,344]{2,3,1,0:T(8,128)(2,1)S(1)}, bf16[1,3,128,344]{2,3,1,0:T(8,128)(2,1)}, u32[]{:S(2)}) copy-start(bf16[1,3,128,344]{2,3,1,0:T(8,128)(2,1)} %copy.226) | copy-start | bytes 792580
  66.4 12.2 %copy-start.4 = (bf16[1,3,128,344]{2,3,1,0:T(8,128)(2,1)S(1)}, bf16[1,3,128,344]{2,3,1,0:T(8,128)(2,1)}, u32[]{:S(2)}) copy-start(bf16[1,3,128,344]{2,3,1,0:T(8,128)(2,1)} %copy.224) | copy-start | bytes 792580
  67.3 11.3 %copy-start.5 = (bf16[1,3,128,344]{2,3,1,0:T(8,128)(2,1)S(1)}, bf16[1,3,128,344]{2,3,1,0:T(8,128)(2,1)}, u32[]{:S(2)}) copy-start(bf16[1,3,128,344]{2,3,1,0:T(8,128)(2,1)} %copy.223) | copy-start | bytes 792580
  69.4 12.4 %copy-start.15 = (bf16[1,3,128,344]{2,3,1,0:T(8,128)(2,1)S(1)}, bf16[1,3,128,344]{2,3,1,0:T(8,128)(2,1)}, u32[]{:S(2)}) copy-start(bf16[1,3,128,344]{2,3,1,0:T(8,128)(2,1)} %copy.230) | copy-start | bytes 792580
  69.4 12.4 %copy-start.14 = (bf16[1,3,128,344]{2,3,1,0:T(8,128)(2,1)S(1)}, bf16[1,3,128,344]{2,3,1,0:T(8,128)(2,1)}, u32[]{:S(2)}) copy-start(bf16[1,3,128,344]{2,3,1,0:T(8,128)(2,1)} %copy.231) | copy-start | bytes 792580
  69.4 12.5 %copy-start.13 = (bf16[1,3,128,344]{2,3,1,0:T(8,128)(2,1)S(1)}, bf16[1,3,128,344]{2,3,1,0:T(8,128)(2,1)}, u32[]{:S(2)}) copy-start(bf16[1,3,128,344]{2,3,1,0:T(8,128)(2,1)} %copy.232) | copy-start | bytes 792580
  69.4 12.5 %copy-start.12 = (bf16[1,3,128,344]{2,3,1,0:T(8,128)(2,1)S(1)}, bf16[1,3,128,344]{2,3,1,0:T(8,128)(2,1)}, u32[]{:S(2)}) copy-start(bf16[1,3,128,344]{2,3,1,0:T(8,128)(2,1)} %copy.233) | copy-start | bytes 792580
  69.4 12.5 %copy-start.11 = (bf16[1,3,128,344]{2,3,1,0:T(8,128)(2,1)S(1)}, bf16[1,3,128,344]{2,3,1,0:T(8,128)(2,1)}, u32[]{:S(2)}) copy-start(bf16[1,3,128,344]{2,3,1,0:T(8,128)(2,1)} %copy.234) | copy-start | bytes 792580
  69.5 12.6 %copy-start.10 = (bf16[1,3,128,344]{2,3,1,0:T(8,128)(2,1)S(1)}, bf16[1,3,128,344]{2,3,1,0:T(8,128)(2,1)}, u32[]{:S(2)}) copy-start(bf16[1,3,128,344]{2,3,1,0:T(8,128)(2,1)} %copy.235) | copy-start | bytes 792580
  69.5 12.6 %copy-start.9 = (bf16[1,3,128,344]{2,3,1,0:T(8,128)(2,1)S(1)}, bf16[1,3,128,344]{2,3,1,0:T(8,128)(2,1)}, u32[]{:S(2)}) copy-start(bf16[1,3,128,344]{2,3,1,0:T(8,128)(2,1)} %copy.236) | copy-start | bytes 792580
  69.5 12.7 %copy-start.8 = (bf16[1,3,128,344]{2,3,1,0:T(8,128)(2,1)S(1)}, bf16[1,3,128,344]{2,3,1,0:T(8,128)(2,1)}, u32[]{:S(2)}) copy-start(bf16[1,3,128,344]{2,3,1,0:T(8,128)(2,1)} %copy.237) | copy-start | bytes 792580
  69.5 12.7 %copy-start.7 = (bf16[1,3,128,344]{2,3,1,0:T(8,128)(2,1)S(1)}, bf16[1,3,128,344]{2,3,1,0:T(8,128)(2,1)}, u32[]{:S(2)}) copy-start(bf16[1,3,128,344]{2,3,1,0:T(8,128)(2,1)} %copy.238) | copy-start | bytes 792580
  69.5 12.8 %copy-start.6 = (bf16[1,3,128,344]{2,3,1,0:T(8,128)(2,1)S(1)}, bf16[1,3,128,344]{2,3,1,0:T(8,128)(2,1)}, u32[]{:S(2)}) copy-start(bf16[1,3,128,344]{2,3,1,0:T(8,128)(2,1)} %copy.239) | copy-start | bytes 792580
  274.9 153.5 %copy-start.1 = (bf16[1,2,4096,128]{3,2,1,0:T(8,128)(2,1)S(1)}, bf16[1,2,4096,128]{3,2,1,0:T(8,128)(2,1)}, u32[]{:S(2)}) copy-start(bf16[1,2,4096,128]{3,2,1,0:T(8,128)(2,1)} %param.5) | copy-start | bytes 6291460
  274.9 176.0 %copy-start.16 = (bf16[4096,4]{0,1:T(4,128)(2,1)S(1)}, bf16[4096,4]{0,1:T(4,128)(2,1)}, u32[]{:S(2)}) copy-start(bf16[4096,4]{0,1:T(4,128)(2,1)} %param.9) | copy-start | bytes 98308
  275.0 153.4 %reduce-scatter.6.cloned.1.call-start = ((), (), s32[]{:S(2)}) async-start(), calls=%async_computation.9 | async-start | bytes 3932160 | tf_op jit(solution)/shard_map/reduce_scatter | solution.py:14
  388.0 64.0 %reduce-scatter.8.cloned.1.call-start = ((), (), s32[]{:S(2)}) async-start(), calls=%async_computation.10 | async-start | bytes 1179648 | tf_op jit(solution)/shard_map/reduce_scatter | solution.py:14
  446.5 29.0 %all-to-all-start = ((bf16[1,2,4096,128]{3,1,0,2:T(2,128)(2,1)}), bf16[1,2,4096,128]{3,1,0,2:T(2,128)(2,1)S(1)}, u32[]{:S(2)}, u32[]{:S(2)}) async-start(bf16[1,2,4096,128]{3,1,0,2:T(2,128)(2,1)} %copy.175), calls=%async_computation | async-start | bytes 4194304 | tf_op jit(solution)/shard_map/all_to_all | solution.py:75
  475.5 12.3 %all-to-all-start.3 = ((bf16[4,12,4096]{2,1,0:T(8,128)(2,1)}), bf16[4,12,4096]{2,1,0:T(8,128)(2,1)S(1)}, u32[]{:S(2)}, u32[]{:S(2)}) async-start(bf16[4,12,4096]{2,1,0:T(8,128)(2,1)} %reshape.55), calls=%async_computation.6 | async-start | bytes 1048576 | tf_op jit(solution)/shard_map/all_to_all | solution.py:68
Sparse Core Ops, SparseCore 0:
  23.0 221.8 all-gather.1
  275.1 112.8 reduce-scatter.3
  390.4 37.9 reduce-scatter.5
  430.6 21.3 reduce-scatter.7
